TPU v7x, 32 devices: a whole 2x2x4 slice. The times are simulated.
32 devices in a mesh: dp: 2 (over x), ep: 16 (over z, y, core).
Axes of the slice: x: 2, y: 2, z: 4, core: 2. Of those that a mesh axis runs over, the one named last changes fastest.
Arguments:
- x_tokens: bfloat16 [16384, 2048], P(('dp', 'ep')), parts along dimension 0
- slot_expert: int32 [80], replicated
- w1_slots: bfloat16 [80, 2048, 1408], P('ep')
- w3_slots: bfloat16 [80, 2048, 1408], P('ep')
- w2_slots: bfloat16 [80, 1408, 2048], P('ep')
- assign: int32 [16384, 6], P(('dp', 'ep')), parts along dimension 0
- w_router: bfloat16 [2048, 64], replicated
- w1_shared: bfloat16 [2048, 2816], replicated
- w3_shared: bfloat16 [2048, 2816], replicated
- w2_shared: bfloat16 [2816, 2048], replicated
Outputs:
- output: bfloat16 [16384, 2048], P(('dp', 'ep')), parts along dimension 0
There are 2 independent parts. A program takes and returns all parts, laid end to end along the dimension named above; an argument that names none is the same for every part.
All inputs are finite; a program needn't handle non-finite values.
Results may differ from a plain program's by a relative error of at most 0.00158.
Values are sent between devices in bfloat16 or wider.
A program may use at most 1 GiB of HBM per device.

v0:
```python
import jax
import jax.numpy as jnp
from jax import lax
from jax.sharding import PartitionSpec as P

ROUTE_SCALE = 2.5


def gate_weights(x_tokens, assign, slot_expert, w_router):
    logits = jnp.dot(x_tokens, w_router, preferred_element_type=jnp.float32)
    gate_prob = jax.nn.sigmoid(logits)
    is_kept = assign >= 0
    chosen = jnp.take(slot_expert, jnp.maximum(assign, 0))
    picked = jnp.where(is_kept, jnp.take_along_axis(gate_prob, chosen, axis=1), 0.0)
    gate_total = jnp.sum(picked, axis=1, keepdims=True)
    return ROUTE_SCALE * picked / jnp.maximum(gate_total, 1e-30), is_kept


def shared_expert(x_tokens, w1_shared, w3_shared, w2_shared):
    h_gate = jnp.dot(x_tokens, w1_shared, preferred_element_type=jnp.float32)
    h_up = jnp.dot(x_tokens, w3_shared, preferred_element_type=jnp.float32)
    mid_act = (jax.nn.silu(h_gate) * h_up).astype(jnp.bfloat16)
    return jnp.dot(mid_act, w2_shared, preferred_element_type=jnp.float32)


def solution(mesh):
    group_size = mesh.shape['ep']

    def device_step(x_tokens, slot_expert, w1_slots, w3_slots, w2_slots, assign, w_router, w1_shared, w3_shared, w2_shared):
        tok_dev, dim_model = x_tokens.shape
        top_k = assign.shape[1]
        local_slots = w1_slots.shape[0]
        num_slots = local_slots * group_size
        cap_rows = max(4, (3 * tok_dev * top_k) // num_slots)
        route_weight, is_kept = gate_weights(x_tokens, assign, slot_expert, w_router)
        shared_out = shared_expert(x_tokens, w1_shared, w3_shared, w2_shared)
        flat_slot = jnp.where(is_kept, assign, num_slots).reshape(-1)
        onehot = (flat_slot[:, None] == jnp.arange(num_slots, dtype=jnp.int32)[None, :]).astype(jnp.int32)
        slot_rank = jnp.sum(jnp.cumsum(onehot, axis=0) * onehot, axis=1) - 1
        dummy_row = num_slots * cap_rows
        row_pos = jnp.where(flat_slot < num_slots, flat_slot * cap_rows + slot_rank, dummy_row)
        token_ids = jnp.arange(tok_dev * top_k, dtype=jnp.int32) // top_k
        row_token = jnp.full((dummy_row + 1,), tok_dev, jnp.int32).at[row_pos].set(token_ids)[:dummy_row]
        send_rows = jnp.take(x_tokens, row_token, axis=0, mode='fill', fill_value=0)
        recv_rows = lax.all_to_all(send_rows, 'ep', 0, 0, tiled=True)
        recv_rows = recv_rows.reshape(group_size, local_slots, cap_rows, dim_model)
        h_gate = jnp.einsum('jlcd,ldf->jlcf', recv_rows, w1_slots, preferred_element_type=jnp.float32)
        h_up = jnp.einsum('jlcd,ldf->jlcf', recv_rows, w3_slots, preferred_element_type=jnp.float32)
        mid_act = (jax.nn.silu(h_gate) * h_up).astype(jnp.bfloat16)
        expert_out = jnp.einsum('jlcf,lfd->jlcd', mid_act, w2_slots, preferred_element_type=jnp.float32).astype(jnp.bfloat16)
        back_rows = lax.all_to_all(expert_out.reshape(dummy_row, dim_model), 'ep', 0, 0, tiled=True)
        gathered = jnp.take(back_rows, jnp.minimum(row_pos, dummy_row - 1), axis=0).reshape(tok_dev, top_k, dim_model)
        routed = jnp.sum(route_weight[:, :, None] * gathered, axis=1)
        return (shared_out + routed).astype(jnp.bfloat16)

    token_spec = P(('dp', 'ep'), None)
    slot_spec = P('ep', None, None)
    return jax.shard_map(device_step, mesh=mesh, in_specs=(token_spec, P(), slot_spec, slot_spec, slot_spec, token_spec, P(), P(), P(), P()), out_specs=token_spec, check_vma=False)
```

profile of v0, /device:TPU:18, one launch (start us, length us, event | category | flops | bytes accessed | tf_op | source)
XLA Modules:
  0.0 2381.5 jit_solution(9075025504056123298)
XLA Ops:
  4.2 39.8 %reduce-window.6 = s32[80,24,128]{2,1,0:T(8,128)S(1)} reduce-window(s32[80,24,128]{2,1,0:T(8,128)} %fusion.21, s32[]{:T(128)} %constant.53.clone.1), window={size=1x1x128 pad=0_0x0_0x127_0}, to_apply=%region_1.2 | reduce-window | flops 31211520 | bytes 1966084 | tf_op jit(solution)/shard_map/reduce-window
  44.0 1.3 slice.23
  45.3 1.7 copy.39
  50.8 11.8 scatter_custom_fusion
  62.6 45.8 %gather_fusion.1 = bf16[9200,2048]{1,0:T(8,128)(2,1)} fusion(bf16[512,2048]{1,0:T(8,128)(2,1)S(1)} %copy-done, s32[9216]{0:T(1024)S(1)} %pad_clamp_fusion), kind=kCustom, calls=%fused_computation.1 | custom fusion | bytes 75403200 | tf_op jit(solution)/shard_map/jit(_take)/gather | solution.py:44
  108.4 36.3 %gather.23 = bf16[16,575,2048]{2,1,0:T(8,128)(2,1)} reshape(bf16[9200,2048]{1,0:T(8,128)(2,1)} %gather_fusion.1) | data formatting | bytes 75366400 | tf_op jit(solution)/shard_map/jit(_take)/gather | solution.py:44
  144.8 25.6 %broadcast_select_fusion = bf16[16,575,2048]{2,1,0:T(8,128)(2,1)} fusion(bf16[16,575,2048]{2,1,0:T(8,128)(2,1)} %gather.23, pred[16,575]{1,0:T(8,128)(4,1)S(1)} %compare_and_fusion.1), kind=kLoop, calls=%fused_computation.13 | loop fusion | flops 18841600 | bytes 75375600 | tf_op jit(solution)/shard_map/jit(_take)/select_n | solution.py:44
  170.4 819.5 %all_to_all.18 = bf16[16,575,2048]{2,1,0:T(8,128)(2,1)} all-to-all(bf16[16,575,2048]{2,1,0:T(8,128)(2,1)} %broadcast_select_fusion), channel_id=1, replica_groups=mesh['dp'=2,'ep'=16] {'ep'}, dimensions={0} | all-to-all | bytes 75366400 | tf_op jit(solution)/shard_map/all_to_all | solution.py:45
  990.0 33.5 %copy.31 = bf16[16,575,2048]{2,0,1:T(8,128)(2,1)} copy(bf16[16,575,2048]{2,1,0:T(8,128)(2,1)} %all_to_all.18) | data formatting | bytes 75366400 | tf_op jit(solution)/shard_map/all_to_all | solution.py:45
  1023.5 120.5 %fusion.4 = f32[5,16,115,1408]{3,2,1,0:T(8,128)} fusion(bf16[16,5,115,2048]{3,0,2,1:T(8,128)(2,1)} %bitcast.70, bf16[5,2048,1408]{2,1,0:T(8,128)(2,1)} %param.13), kind=kOutput, calls=%fused_computation.14 | convolution fusion | flops 53057945600 | bytes 118333440 | tf_op jit(solution)/shard_map/jlcd,ldf->jlcf/dot_general | solution.py:48
  1144.0 105.8 %fusion = bf16[16,5,115,1408]{3,2,0,1:T(8,128)(2,1)} fusion(f32[5,16,115,1408]{3,2,1,0:T(8,128)} %fusion.4, bf16[16,5,115,2048]{3,0,2,1:T(8,128)(2,1)} %bitcast.71, bf16[5,2048,1408]{2,1,0:T(8,128)(2,1)} %param.12), kind=kOutput, calls=%fused_computation.6 | convolution fusion | flops 53135654912 | bytes 144240640 | tf_op jit(solution)/shard_map/jlcd,ldf->jlcf/dot_general | solution.py:47
  1249.9 70.4 %convert_bitcast_fusion = bf16[16,5,115,2048]{3,2,0,1:T(8,128)(2,1)} fusion(bf16[16,5,115,1408]{3,2,0,1:T(8,128)(2,1)} %fusion, bf16[5,1408,2048]{2,1,0:T(8,128)(2,1)} %param.14), kind=kOutput, calls=%fused_computation.12 | convolution fusion | flops 53076787200 | bytes 92426240 | tf_op jit(solution)/shard_map/jlcf,lfd->jlcd/dot_general | solution.py:50
  1320.3 34.7 %copy.34 = bf16[16,5,115,2048]{3,0,2,1:T(8,128)(2,1)} copy(bf16[16,5,115,2048]{3,2,0,1:T(8,128)(2,1)} %convert_bitcast_fusion) | data formatting | bytes 75366400 | tf_op jit(solution)/shard_map/convert_element_type | solution.py:50
  1355.0 33.7 %copy.35 = bf16[16,575,2048]{2,1,0:T(8,128)(2,1)} copy(bf16[16,575,2048]{2,0,1:T(8,128)(2,1)} %bitcast.69) | data formatting | bytes 75366400 | tf_op jit(solution)/shard_map/all_to_all | solution.py:51
  1388.7 6.5 all-to-all-start.1
  1395.9 18.7 gather_fusion
  1415.9 24.9 %gather_fusion.3 = f32[3072]{0:T(1024)S(1)} fusion(f32[512,64]{0,1:T(8,128)S(1)} %fusion.18, s32[3072]{0:T(1024)S(1)} %reshape.176), kind=kCustom, calls=%fused_computation.3 | custom fusion | bytes 49152 | tf_op jit(solution)/shard_map/jit(take_along_axis)/gather | solution.py:14
  1441.4 11.2 fusion.30
  1452.7 754.8 %all-to-all-done.1 = bf16[16,575,2048]{2,1,0:T(8,128)(2,1)} async-done(((bf16[16,575,2048]{2,1,0:T(8,128)(2,1)}), bf16[16,575,2048]{2,1,0:T(8,128)(2,1)}, u32[]{:S(2)}, u32[]{:S(2)}) %all-to-all-start.1) | async-done | bytes 37683232 | tf_op jit(solution)/shard_map/all_to_all | solution.py:51
  2207.5 36.3 %all_to_all.15 = bf16[9200,2048]{1,0:T(8,128)(2,1)} reshape(bf16[16,575,2048]{2,1,0:T(8,128)(2,1)} %all-to-all-done.1) | data formatting | bytes 75366400 | tf_op jit(solution)/shard_map/all_to_all | solution.py:51
  2243.8 72.1 %gather_fusion.2 = bf16[3072,2048]{1,0:T(8,128)(2,1)} fusion(bf16[9200,2048]{1,0:T(8,128)(2,1)} %all_to_all.15, s32[3072]{0:T(1024)S(1)} %broadcast_clamp_fusion), kind=kCustom, calls=%fused_computation.2 | custom fusion | bytes 25178112 | tf_op jit(solution)/shard_map/jit(_take)/gather | solution.py:52
  2315.8 20.5 gather.25
  2336.3 21.0 multiply_reduce_fusion
  2357.3 23.9 %add_convert_fusion = bf16[512,2048]{1,0:T(8,128)(2,1)} fusion(f32[512,2048]{1,0:T(8,128)} %multiply_reduce_fusion, bf16[2816,2048]{1,0:T(8,128)(2,1)} %param.19, f32[512,2816]{1,0:T(8,128)} %fusion.30, bf16[512,2048]{1,0:T(8,128)(2,1)S(1)} %copy-done, bf16[2048,2816]{1,0:T(8,128)(2,1)} %param.18), kind=kOutput, calls=%fused_computation.24 | convolution fusion | flops 11821907968 | bytes 37224448 | tf_op jit(solution)/shard_map/dot_general | solution.py:23
  (52 shorter events, 10.5 us)
Async XLA Ops:
  0.0 62.6 %copy-start = (bf16[512,2048]{1,0:T(8,128)(2,1)S(1)}, bf16[512,2048]{1,0:T(8,128)(2,1)}, u32[]{:S(2)}) copy-start(bf16[512,2048]{1,0:T(8,128)(2,1)} %param.10) | copy-start | bytes 6291460
  1.0 2.2 copy-start.2
  2.0 1.2 copy-start.5
  1388.7 6.6 copy-start.4
  1388.7 818.8 %all-to-all-start.1 = ((bf16[16,575,2048]{2,1,0:T(8,128)(2,1)}), bf16[16,575,2048]{2,1,0:T(8,128)(2,1)}, u32[]{:S(2)}, u32[]{:S(2)}) async-start(bf16[16,575,2048]{2,1,0:T(8,128)(2,1)} %copy.35), calls=%async_computation.1 | async-start | bytes 75497472 | tf_op jit(solution)/shard_map/all_to_all | solution.py:51
  1395.2 0.7 copy-start.1
  1395.9 18.9 copy-start.3
  1395.9 19.2 copy-start.9
  1415.9 25.2 %copy-start.6 = (pred[512,6]{1,0:T(8,128)(4,1)S(1)}, pred[512,6]{1,0:T(8,128)(4,1)}, u32[]{:S(2)}) copy-start(pred[512,6]{1,0:T(8,128)(4,1)} %copy-done.5) | copy-start | bytes 9220
  1415.9 25.4 %copy-start.8 = (s32[3072,1]{0,1:T(1,128)S(1)}, s32[3072,1]{0,1:T(1,128)}, u32[]{:S(2)}) copy-start(s32[3072,1]{0,1:T(1,128)} %get-tuple-element.12) | copy-start | bytes 36868
  2315.8 20.5 copy-start.7
where the time goes:
time: 2400 us; the launch traced here: 2380 us
  blocking collectives  820 us (34%)
  waiting for transfers between devices  755 us (31%)
  local copies, waits for them, and re-layouts  376 us (16%)
  matrix products  333 us (14%)
  other arithmetic  91.7 us (4%)
    all_to_all x1, blocking collectives, device_step(): recv_rows = lax.all_to_all(send_rows, 'ep', 0, 0, tiled=True)  820 us
    all_to_all x1, waiting for transfers between devices, device_step(): lax.all_to_all(expert_out.reshape(dummy_row, dim_model), 'ep', 0, 0, tile...  755 us
    dot_general x1, matrix products, device_step(): jnp.einsum('jlcd,ldf->jlcf', recv_rows, w3_slots, preferred_element_type=...  121 us
    dot_general x1, matrix products, device_step(): jnp.einsum('jlcd,ldf->jlcf', recv_rows, w1_slots, preferred_element_type=...  106 us
    gather x2, local copies, waits for them, and re-layouts, device_step(): jnp.take(back_rows, jnp.minimum(row_pos, dummy_row - 1), axis=0)  92.6 us
    gather x2, local copies, waits for them, and re-layouts, device_step(): send_rows = jnp.take(x_tokens, row_token, axis=0, mode='fill', fill_value=0)  82.1 us
    dot_general x1, matrix products, device_step(): jnp.einsum('jlcf,lfd->jlcd', mid_act, w2_slots, preferred_element_type=jn...  70.4 us
    all_to_all x2, local copies, waits for them, and re-layouts, device_step(): lax.all_to_all(expert_out.reshape(dummy_row, dim_model), 'ep', 0, 0, tile...  70 us
  transfers between devices with their start and end apart: 1, of which 1 were waited for; matrix products, arithmetic and copies ran while one was open for 2% of the time, Pallas kernels for 0%

commit v1 on v0

v1 whole, which is shorter than its diff:
```python
import jax
import jax.numpy as jnp
from jax import lax
from jax.experimental import pallas as pl
from jax.experimental.pallas import tpu as pltpu
from jax.sharding import PartitionSpec as P

ROUTE_SCALE = 2.5
TM = 256
WIN = 128
ALIGN = 16


def gate_weights(x_tokens, assign, slot_expert, w_router):
    logits = jnp.dot(x_tokens, w_router, preferred_element_type=jnp.float32)
    gate_prob = jax.nn.sigmoid(logits)
    is_kept = assign >= 0
    chosen = jnp.take(slot_expert, jnp.maximum(assign, 0))
    hit = chosen[:, :, None] == jnp.arange(gate_prob.shape[1], dtype=jnp.int32)
    picked = jnp.sum(jnp.where(hit, gate_prob[:, None, :], 0.0), axis=2)
    picked = jnp.where(is_kept, picked, 0.0)
    gate_total = jnp.sum(picked, axis=1, keepdims=True)
    return ROUTE_SCALE * picked / jnp.maximum(gate_total, 1e-30)


def shared_expert(x_tokens, w1_shared, w3_shared, w2_shared):
    h_gate = jnp.dot(x_tokens, w1_shared, preferred_element_type=jnp.float32)
    h_up = jnp.dot(x_tokens, w3_shared, preferred_element_type=jnp.float32)
    mid_act = (jax.nn.silu(h_gate) * h_up).astype(jnp.bfloat16)
    return jnp.dot(mid_act, w2_shared, preferred_element_type=jnp.float32)


def dispatch(x_all, rank_rows, off, cpad, tail, max_rows):
    blocks, _, tok = rank_rows.shape
    slots = tail.shape[0]
    dim = x_all.shape[1]

    def kernel(off_ref, cpad_ref, tail_ref, rank_ref, x_ref, out_ref, stage, zeros, sem, zsem):
        b = pl.program_id(0)
        buf = lax.rem(b, 2)

        def copy16(i, src_row, dst_row):
            return pltpu.make_async_copy(
                stage.at[i, pl.ds(pl.multiple_of(src_row, ALIGN), ALIGN), :],
                out_ref.at[pl.ds(pl.multiple_of(dst_row, ALIGN), ALIGN), :],
                sem.at[i],
            )

        def drain(step, i):
            total = cpad_ref[step * slots]
            for s in range(1, slots):
                total = total + cpad_ref[step * slots + s]

            def body(_, c):
                copy16(i, 0, 0).wait()
                return c

            lax.fori_loop(0, lax.div(total, ALIGN), body, 0)

        @pl.when(b >= 2)
        def _():
            drain(b - 2, buf)

        rows = lax.broadcasted_iota(jnp.int32, (WIN, tok), 0)
        sel = [(rows == rank_ref[0, s : s + 1, :]).astype(jnp.float32).astype(jnp.bfloat16) for s in range(slots)]
        win = jnp.dot(jnp.concatenate(sel, axis=0), x_ref[...], preferred_element_type=jnp.float32)
        stage[buf] = win.astype(jnp.bfloat16)
        for s in range(slots):
            start = off_ref[b * slots + s]

            def body(c, carry):
                copy16(buf, s * WIN + c * ALIGN, start + c * ALIGN).start()
                return carry

            lax.fori_loop(0, lax.div(cpad_ref[b * slots + s], ALIGN), body, 0)

        @pl.when(b == blocks - 1)
        def _():
            zeros[...] = jnp.zeros_like(zeros)

            def zcopy(row):
                return pltpu.make_async_copy(zeros, out_ref.at[pl.ds(pl.multiple_of(row, ALIGN), ALIGN), :], zsem)

            for wait in (False, True):
                for s in range(slots):
                    first = off_ref[b * slots + s] + cpad_ref[b * slots + s]

                    def body(c, carry):
                        d = zcopy(first + c * ALIGN)
                        d.wait() if wait else d.start()
                        return carry

                    lax.fori_loop(0, lax.div(tail_ref[s] - first, ALIGN), body, 0)
            drain(b - 1, 1 - buf)
            drain(b, buf)

    return pl.pallas_call(
        kernel,
        grid_spec=pltpu.PrefetchScalarGridSpec(
            num_scalar_prefetch=3,
            grid=(blocks,),
            in_specs=[
                pl.BlockSpec((1, rank_rows.shape[1], tok), lambda b, *_: (b, 0, 0)),
                pl.BlockSpec((tok, dim), lambda b, *_: (b, 0)),
            ],
            out_specs=pl.BlockSpec(memory_space=pl.ANY),
            scratch_shapes=[
                pltpu.VMEM((2, slots * WIN, dim), jnp.bfloat16),
                pltpu.VMEM((ALIGN, dim), jnp.bfloat16),
                pltpu.SemaphoreType.DMA((2,)),
                pltpu.SemaphoreType.DMA,
            ],
        ),
        out_shape=jax.ShapeDtypeStruct((max_rows, dim), jnp.bfloat16),
        compiler_params=pltpu.CompilerParams(vmem_limit_bytes=48 * 2**20),
        name="dispatch",
    )(off, cpad, tail, rank_rows, x_all)


def expert_mlp(x_rows, w1, w3, w2, tile_slot, num_tiles):
    dim, ff = w1.shape[1:]

    def kernel(slot_ref, tiles_ref, x_ref, w1_ref, w3_ref, w2_ref, o_ref):
        @pl.when(pl.program_id(0) < tiles_ref[0])
        def _():
            x = x_ref[...]
            gate = jnp.dot(x, w1_ref[0], preferred_element_type=jnp.float32)
            up = jnp.dot(x, w3_ref[0], preferred_element_type=jnp.float32)
            mid = (jax.nn.silu(gate) * up).astype(jnp.bfloat16)
            o_ref[...] = jnp.dot(mid, w2_ref[0], preferred_element_type=jnp.float32).astype(jnp.bfloat16)

    def row_block(i, slot, tiles):
        return jnp.minimum(i, tiles[0] - 1), 0

    return pl.pallas_call(
        kernel,
        grid_spec=pltpu.PrefetchScalarGridSpec(
            num_scalar_prefetch=2,
            grid=(x_rows.shape[0] // TM,),
            in_specs=[
                pl.BlockSpec((TM, dim), row_block),
                pl.BlockSpec((1, dim, ff), lambda i, slot, tiles: (slot[i], 0, 0)),
                pl.BlockSpec((1, dim, ff), lambda i, slot, tiles: (slot[i], 0, 0)),
                pl.BlockSpec((1, ff, dim), lambda i, slot, tiles: (slot[i], 0, 0)),
            ],
            out_specs=pl.BlockSpec((TM, dim), row_block),
        ),
        out_shape=jax.ShapeDtypeStruct(x_rows.shape, jnp.bfloat16),
        compiler_params=pltpu.CompilerParams(vmem_limit_bytes=60 * 2**20),
        name="expert_mlp",
    )(tile_slot, num_tiles.reshape(1), x_rows, w1, w3, w2)


def combine(o_rows, rank_cols, w_cols, win_start):
    blocks, tok, slots = rank_cols.shape
    dim = o_rows.shape[1]

    def kernel(start_ref, rank_ref, w_ref, o_ref, out_ref, wins, sem):
        b = pl.program_id(0)
        buf = lax.rem(b, 2)

        def fetch(step, i):
            return [
                pltpu.make_async_copy(
                    o_ref.at[pl.ds(pl.multiple_of(start_ref[step * slots + s], ALIGN), WIN), :],
                    wins.at[i, pl.ds(s * WIN, WIN), :],
                    sem.at[i, s],
                )
                for s in range(slots)
            ]

        @pl.when(b == 0)
        def _():
            for c in fetch(b, buf):
                c.start()

        @pl.when(b + 1 < blocks)
        def _():
            for c in fetch(b + 1, 1 - buf):
                c.start()

        lanes = lax.broadcasted_iota(jnp.int32, (tok, WIN), 1)
        a = jnp.concatenate(
            [jnp.where(lanes == rank_ref[0, :, s : s + 1], w_ref[0, :, s : s + 1], 0.0) for s in range(slots)], axis=1
        )
        hi = a.astype(jnp.bfloat16)
        rest = a - hi.astype(jnp.float32)
        mid = rest.astype(jnp.bfloat16)
        low = (rest - mid.astype(jnp.float32)).astype(jnp.bfloat16)
        for c in fetch(b, buf):
            c.wait()
        o = wins[buf]
        acc = jnp.dot(hi, o, preferred_element_type=jnp.float32)
        acc += jnp.dot(mid, o, preferred_element_type=jnp.float32)
        acc += jnp.dot(low, o, preferred_element_type=jnp.float32)
        out_ref[...] = acc

    return pl.pallas_call(
        kernel,
        grid_spec=pltpu.PrefetchScalarGridSpec(
            num_scalar_prefetch=1,
            grid=(blocks,),
            in_specs=[
                pl.BlockSpec((1, tok, slots), lambda b, *_: (b, 0, 0)),
                pl.BlockSpec((1, tok, slots), lambda b, *_: (b, 0, 0)),
                pl.BlockSpec(memory_space=pl.ANY),
            ],
            out_specs=pl.BlockSpec((tok, dim), lambda b, *_: (b, 0)),
            scratch_shapes=[
                pltpu.VMEM((2, slots * WIN, dim), jnp.bfloat16),
                pltpu.SemaphoreType.DMA((2, slots)),
            ],
        ),
        out_shape=jax.ShapeDtypeStruct((blocks * tok, dim), jnp.float32),
        compiler_params=pltpu.CompilerParams(vmem_limit_bytes=56 * 2**20),
        name="combine",
    )(win_start, rank_cols, w_cols, o_rows)


def routing_plan(assign_all, weight_all, first_slot, slots):
    blocks, tok, _ = assign_all.shape
    hit = (assign_all - first_slot)[..., None] == jnp.arange(slots, dtype=jnp.int32)
    member = jnp.any(hit, axis=2)
    weight = jnp.sum(jnp.where(hit, weight_all[..., None], 0.0), axis=2)
    upto = (jnp.arange(tok)[:, None] >= jnp.arange(tok)[None, :]).astype(jnp.bfloat16)
    order = jnp.einsum('pq,bqs->bps', upto, member.astype(jnp.bfloat16), preferred_element_type=jnp.float32)
    order = order.astype(jnp.int32)
    count = order[:, -1, :]
    rank = jnp.where(member, order - 1, -4 * WIN)
    cpad = (count + ALIGN - 1) // ALIGN * ALIGN
    inside = jnp.cumsum(cpad, axis=0) - cpad
    tiles = (jnp.sum(cpad, axis=0) + TM - 1) // TM
    tile_end = jnp.cumsum(tiles)
    off = ((tile_end - tiles) * TM)[None, :] + inside
    return rank, weight, cpad, off, tile_end


def solution(mesh):
    group_size = mesh.shape['ep']

    def device_step(x_tokens, slot_expert, w1_slots, w3_slots, w2_slots, assign, w_router, w1_shared, w3_shared, w2_shared):
        tok, dim = x_tokens.shape
        top_k = assign.shape[1]
        slots = w1_slots.shape[0]
        me = lax.axis_index('ep')
        max_tiles = slots * (group_size * WIN // TM)
        weight = gate_weights(x_tokens, assign, slot_expert, w_router)
        meta = lax.all_gather(jnp.concatenate([assign.astype(jnp.float32), weight], axis=1), 'ep')
        x_all = lax.all_gather(x_tokens, 'ep', tiled=True)
        shared_out = shared_expert(x_tokens, w1_shared, w3_shared, w2_shared)
        rank, w_all, cpad, off, tile_end = routing_plan(
            meta[..., :top_k].astype(jnp.int32), meta[..., top_k:], me * slots, slots
        )
        num_tiles = jnp.maximum(tile_end[-1], 1)
        tile_ids = jnp.arange(max_tiles, dtype=jnp.int32)
        tile_slot = jnp.sum((jnp.minimum(tile_ids, num_tiles - 1)[:, None] >= tile_end[None, :-1]).astype(jnp.int32), axis=1)
        tail = (tile_end * TM).at[-1].set(num_tiles * TM)
        rank_rows = jnp.pad(jnp.transpose(rank, (0, 2, 1)), ((0, 0), (0, 8 - slots), (0, 0)), constant_values=-1)
        x_rows = dispatch(x_all, rank_rows, off.reshape(-1), cpad.reshape(-1), tail, max_tiles * TM)
        o_rows = expert_mlp(x_rows, w1_slots, w3_slots, w2_slots, tile_slot, num_tiles)
        win_start = jnp.minimum(off, num_tiles * TM - WIN)
        partial = combine(o_rows, rank + (off - win_start)[:, None, :], w_all, win_start.reshape(-1))
        routed = lax.psum_scatter(partial, 'ep', scatter_dimension=0, tiled=True)
        return (shared_out + routed).astype(jnp.bfloat16)

    token_spec = P(('dp', 'ep'), None)
    slot_spec = P('ep', None, None)
    return jax.shard_map(device_step, mesh=mesh, in_specs=(token_spec, P(), slot_spec, slot_spec, slot_spec, token_spec, P(), P(), P(), P()), out_specs=token_spec, check_vma=False)
```

time: 2400 us -> 1110 us (0.46)
  the two profiles are of different devices: /device:TPU:18 before, /device:TPU:1 now
where the time goes in v1:
time: 1110 us; the launch traced here: 1100 us
  waiting for transfers between devices  719 us (65%)
  Pallas kernels  241 us (22%)
  local copies, waits for them, and re-layouts  39.8 us (4%)
  matrix products  36.8 us (3%)
  blocking collectives  27.2 us (2%)
  other arithmetic  20.4 us (2%)
  between operations  14.3 us (1%)
    reduce_scatter x1, waiting for transfers between devices, device_step(): routed = lax.psum_scatter(partial, 'ep', scatter_dimension=0, tiled=True)  632 us
    pallas_call x1, Pallas kernels, expert_mlp(): pl.pallas_call(kernel, grid_spec=pltpu.PrefetchScalarGridSpec(num_scalar_...  109 us
    pallas_call x1, Pallas kernels, combine(): pl.pallas_call(kernel, grid_spec=pltpu.PrefetchScalarGridSpec(num_scalar_...  98.7 us
    all_gather x1, waiting for transfers between devices, device_step(): x_all = lax.all_gather(x_tokens, 'ep', tiled=True)  86.6 us
    pallas_call x1, Pallas kernels, dispatch(): pl.pallas_call(kernel, grid_spec=pltpu.PrefetchScalarGridSpec(num_scalar_...  32.8 us
    all_gather x1, blocking collectives, device_step(): lax.all_gather(jnp.concatenate([assign.astype(jnp.float32), weight], axis...  27.2 us
    dot_general x1, matrix products, shared_expert(): return jnp.dot(mid_act, w2_shared, preferred_element_type=jnp.float32)  24 us
  transfers between devices with their start and end apart: 2, of which 2 were waited for; matrix products, arithmetic and copies ran while one was open for 6% of the time, Pallas kernels for 0%

profile of v1, /device:TPU:1, one launch (start us, length us, event | category | flops | bytes accessed | tf_op | source)
XLA Modules:
  0.0 1098.7 jit_solution(9544982373166067409)
XLA Ops:
  7.3 0.7 broadcast_maximum_fusion
  8.4 18.7 %gather_fusion = s32[3072]{0:T(1024)S(1)} fusion(s32[80]{0:T(128)S(1)} %copy-done.2, s32[3072]{0:T(1024)S(1)} %broadcast_clamp_fusion), kind=kCustom, calls=%fused_computation | custom fusion | bytes 36864 | tf_op jit(solution)/shard_map/jit(_take)/gather | solution.py:18
  27.4 0.8 fusion.2
  28.4 27.2 %all-gather = f32[8192,12]{0,1:T(8,128)S(1)} all-gather(f32[512,12]{0,1:T(8,128)S(1)} %pad_maximum_fusion), channel_id=2, replica_groups=mesh['dp'=2,'ep'=16] {'ep'}, dimensions={0}, use_global_device_ids=true | all-gather | bytes 417792 | tf_op jit(solution)/shard_map/all_gather | solution.py:248
  56.9 1.8 copy.84
  58.6 0.9 fusion.4
  59.5 3.5 copy.73
  63.1 2.6 convert_bitcast_fusion
  65.7 2.0 copy-done.3
  69.6 0.9 minimum_subtract_fusion
  70.7 5.0 add_select_fusion
  75.7 2.8 copy.91
  78.5 4.7 broadcast_add_fusion
  83.2 2.9 copy.77
  86.2 2.6 copy.83
  88.9 2.7 copy.86.w_ref
  92.8 4.5 broadcast_add_fusion.1.rank_ref
  97.3 86.6 %all-gather.3.cloned.1.call-done.x_ref = bf16[8192,2048]{1,0:T(8,128)(2,1)} async-done(((bf16[512,2048]{1,0:T(8,128)(2,1)}), bf16[8192,2048]{1,0:T(8,128)(2,1)}) %all-gather.3.cloned.1.call-update) | async-done | bytes 33554448 | tf_op jit(solution)/shard_map/all_gather | solution.py:249
  183.9 32.8 %dispatch.1.x_ref = bf16[10240,2048]{1,0:T(8,128)(2,1)} custom-call(s32[80]{0:T(128)S(1)} %get-tuple-element.18.off_ref, s32[80]{0:T(128)S(1)} %get-tuple-element.19.cpad_ref, s32[5]{0:T(128)S(1)} %bitcast_dynamic-update-slice_fusion.tail_ref, s32[16,8,512]{2,1,0:T(8,128)S(1)} %pad.6.clone.rank_ref, bf16[8192,2048]{1,0:T(8,128)(2,1)} %all-gather.3.cloned.1.call-done.x_ref), custom_call_target="tpu_custom_call" | custom-call | tf_op jit(solution)/shard_map/dispatch/pallas_call | solution.py:97
  216.7 109.5 %expert_mlp.1.o_ref = bf16[10240,2048]{1,0:T(8,128)(2,1)} custom-call(s32[40]{0:T(128)} %convert_reduce_fusion.slot_ref, s32[1]{0:T(128)} %bitcast.10.tiles_ref, bf16[10240,2048]{1,0:T(8,128)(2,1)} %dispatch.1.x_ref, bf16[5,2048,1408]{2,1,0:T(8,128)(2,1)} %w1_ref.1, bf16[5,2048,1408]{2,1,0:T(8,128)(2,1)} %w3_ref.1, bf16[5,1408,2048]{2,1,0:T(8,128)(2,1)} %w2_ref.1), custom_call_target="tpu_custom_call" | custom-call | tf_op jit(solution)/shard_map/expert_mlp/pallas_call | solution.py:135
  326.2 98.7 %combine.1 = f32[8192,2048]{1,0:T(8,128)} custom-call(s32[80]{0:T(128)} %get-tuple-element.17.start_ref, s32[16,512,5]{2,1,0:T(8,128)} %broadcast_add_fusion.1.rank_ref, f32[16,512,5]{2,1,0:T(8,128)} %copy.86.w_ref, bf16[10240,2048]{1,0:T(8,128)(2,1)} %expert_mlp.1.o_ref), custom_call_target="tpu_custom_call" | custom-call | tf_op jit(solution)/shard_map/combine/pallas_call | solution.py:198
  425.0 11.1 %fusion.21 = f32[512,2816]{1,0:T(8,128)} fusion(bf16[512,2048]{1,0:T(8,128)(2,1)S(1)} %copy-done.4, bf16[2048,2816]{1,0:T(8,128)(2,1)} %param.19), kind=kOutput, calls=%fused_computation.74 | convolution fusion | flops 5905580032 | bytes 19398656 | tf_op jit(solution)/shard_map/dot_general | solution.py:27
  436.1 631.8 %reduce-scatter.2.cloned.1.call-done = f32[512,2048]{1,0:T(8,128)} async-done(((f32[8192,2048]{1,0:T(8,128)}), f32[512,2048]{1,0:T(8,128)}) %reduce-scatter.2.cloned.1.call-update) | async-done | bytes 4194320 | tf_op jit(solution)/shard_map/reduce_scatter | solution.py:263
  1067.9 24.0 %add_convert_fusion = bf16[512,2048]{1,0:T(8,128)(2,1)} fusion(f32[512,2048]{1,0:T(8,128)} %reduce-scatter.2.cloned.1.call-done, bf16[2816,2048]{1,0:T(8,128)(2,1)} %param.21, f32[512,2816]{1,0:T(8,128)} %fusion.21, bf16[512,2048]{1,0:T(8,128)(2,1)S(1)} %copy-done.4, bf16[2048,2816]{1,0:T(8,128)(2,1)} %param.20), kind=kOutput, calls=%fused_computation.2 | convolution fusion | flops 11821907968 | bytes 37224448 | tf_op jit(solution)/shard_map/dot_general | solution.py:30
  (55 shorter events, 5.6 us)
Async XLA Ops:
  6.5 20.9 %copy-start = (bf16[2048,64]{0,1:T(8,128)(2,1)S(1)}, bf16[2048,64]{0,1:T(8,128)(2,1)}, u32[]{:S(2)}) copy-start(bf16[2048,64]{0,1:T(8,128)(2,1)} %param.18) | copy-start | bytes 786436
  6.5 1.8 copy-start.2
  6.5 177.4 %all-gather.3.cloned.1.call-start = ((), (), s32[]{:S(2)}) async-start(), calls=%async_computation.1 | async-start | bytes 35651584 | tf_op jit(solution)/shard_map/all_gather | solution.py:249
  7.3 1060.6 %reduce-scatter.2.cloned.1.call-start = ((), (), s32[]{:S(2)}) async-start(), calls=%async_computation.2 | async-start | bytes 71303168 | tf_op jit(solution)/shard_map/reduce_scatter | solution.py:263
  8.4 19.0 %copy-start.6 = (s32[512,6]{0,1:T(8,128)S(1)}, s32[512,6]{0,1:T(8,128)}, u32[]{:S(2)}) copy-start(s32[512,6]{0,1:T(8,128)} %param.17) | copy-start | bytes 36868
  8.4 19.0 %copy-start.4 = (bf16[512,2048]{1,0:T(8,128)(2,1)S(1)}, bf16[512,2048]{1,0:T(8,128)(2,1)}, u32[]{:S(2)}) copy-start(bf16[512,2048]{1,0:T(8,128)(2,1)} %param.12) | copy-start | bytes 6291460
  56.0 0.7 copy-start.5
  65.6 2.0 copy-start.3
  83.2 5.6 slice-start
  1067.9 24.0 %copy-start.1 = (bf16[2048,64]{0,1:T(8,128)(2,1)S(1)}, bf16[2048,64]{0,1:T(8,128)(2,1)}, u32[]{:S(2)}) copy-start(bf16[2048,64]{0,1:T(8,128)(2,1)} %param.18) | copy-start | bytes 786436
Sparse Core Ops, SparseCore 0:
  8.9 174.9 all-gather.2
  425.1 642.7 reduce-scatter.1

commit v2 on v1

v2 whole, which is shorter than its diff:
```python
import jax
import jax.numpy as jnp
from jax import lax
from jax.experimental import pallas as pl
from jax.experimental.pallas import tpu as pltpu
from jax.sharding import PartitionSpec as P

ROUTE_SCALE = 2.5
TM = 256
WIN = 128
ALIGN = 16
CAP = 384
PIECE = 512
MESH = pl.DeviceIdType.MESH


def gate_weights(x_tokens, assign, slot_expert, w_router):
    num_experts, num_slots = w_router.shape[1], slot_expert.shape[0]
    pick = (jnp.arange(num_experts, dtype=jnp.int32)[:, None] == slot_expert[None, :]).astype(w_router.dtype)
    w_slot = jnp.dot(w_router, pick)
    gate_prob = jax.nn.sigmoid(jnp.dot(x_tokens, w_slot, preferred_element_type=jnp.float32))
    hit = assign[:, :, None] == jnp.arange(num_slots, dtype=jnp.int32)
    picked = jnp.sum(jnp.where(hit, gate_prob[:, None, :], 0.0), axis=2)
    gate_total = jnp.sum(picked, axis=1, keepdims=True)
    return ROUTE_SCALE * picked / jnp.maximum(gate_total, 1e-30)


def shared_expert(x_tokens, w1_shared, w3_shared, w2_shared):
    h_gate = jnp.dot(x_tokens, w1_shared, preferred_element_type=jnp.float32)
    h_up = jnp.dot(x_tokens, w3_shared, preferred_element_type=jnp.float32)
    mid_act = (jax.nn.silu(h_gate) * h_up).astype(jnp.bfloat16)
    return jnp.dot(mid_act, w2_shared, preferred_element_type=jnp.float32)


def dispatch(x_all, rank_rows, off, cpad, tail, max_rows):
    blocks, _, tok = rank_rows.shape
    slots = tail.shape[0]
    dim = x_all.shape[1]

    def kernel(off_ref, cpad_ref, tail_ref, rank_ref, x_ref, out_ref, stage, zeros, sem, zsem):
        b = pl.program_id(0)
        buf = lax.rem(b, 2)

        def copy16(i, src_row, dst_row):
            return pltpu.make_async_copy(
                stage.at[i, pl.ds(pl.multiple_of(src_row, ALIGN), ALIGN), :],
                out_ref.at[pl.ds(pl.multiple_of(dst_row, ALIGN), ALIGN), :],
                sem.at[i],
            )

        def drain(step, i):
            total = cpad_ref[step * slots]
            for s in range(1, slots):
                total = total + cpad_ref[step * slots + s]

            def body(_, c):
                copy16(i, 0, 0).wait()
                return c

            lax.fori_loop(0, lax.div(total, ALIGN), body, 0)

        @pl.when(b >= 2)
        def _():
            drain(b - 2, buf)

        rows = lax.broadcasted_iota(jnp.int32, (WIN, tok), 0)
        sel = [(rows == rank_ref[0, s : s + 1, :]).astype(jnp.float32).astype(jnp.bfloat16) for s in range(slots)]
        win = jnp.dot(jnp.concatenate(sel, axis=0), x_ref[...], preferred_element_type=jnp.float32)
        stage[buf] = win.astype(jnp.bfloat16)
        for s in range(slots):
            start = off_ref[b * slots + s]

            def body(c, carry):
                copy16(buf, s * WIN + c * ALIGN, start + c * ALIGN).start()
                return carry

            lax.fori_loop(0, lax.div(cpad_ref[b * slots + s], ALIGN), body, 0)

        @pl.when(b == blocks - 1)
        def _():
            zeros[...] = jnp.zeros_like(zeros)

            def zcopy(row):
                return pltpu.make_async_copy(zeros, out_ref.at[pl.ds(pl.multiple_of(row, ALIGN), ALIGN), :], zsem)

            for wait in (False, True):
                for s in range(slots):
                    first = off_ref[b * slots + s] + cpad_ref[b * slots + s]

                    def body(c, carry):
                        d = zcopy(first + c * ALIGN)
                        d.wait() if wait else d.start()
                        return carry

                    lax.fori_loop(0, lax.div(tail_ref[s] - first, ALIGN), body, 0)
            drain(b - 1, 1 - buf)
            drain(b, buf)

    return pl.pallas_call(
        kernel,
        grid_spec=pltpu.PrefetchScalarGridSpec(
            num_scalar_prefetch=3,
            grid=(blocks,),
            in_specs=[
                pl.BlockSpec((1, rank_rows.shape[1], tok), lambda b, *_: (b, 0, 0)),
                pl.BlockSpec((tok, dim), lambda b, *_: (b, 0)),
            ],
            out_specs=pl.BlockSpec(memory_space=pl.ANY),
            scratch_shapes=[
                pltpu.VMEM((2, slots * WIN, dim), jnp.bfloat16),
                pltpu.VMEM((ALIGN, dim), jnp.bfloat16),
                pltpu.SemaphoreType.DMA((2,)),
                pltpu.SemaphoreType.DMA,
            ],
        ),
        out_shape=jax.ShapeDtypeStruct((max_rows, dim), jnp.bfloat16),
        compiler_params=pltpu.CompilerParams(vmem_limit_bytes=48 * 2**20),
        name="dispatch",
    )(off, cpad, tail, rank_rows, x_all)


def expert_mlp(x_rows, w1, w3, w2, tile_slot, num_tiles, chunk_dst, chunk_count, used, out_rows):
    dim, ff = w1.shape[1:]
    tiles_max = x_rows.shape[0] // TM
    chunks = TM // ALIGN
    parts = out_rows // CAP

    def kernel(slot_ref, tiles_ref, dst_ref, count_ref, used_ref, x_ref, w1_ref, w3_ref, w2_ref, o_ref, stage, zeros, sem, zsem):
        i = pl.program_id(0)
        buf = lax.rem(i, 2)
        tiles = tiles_ref[0]

        def copy16(k, c, row):
            return pltpu.make_async_copy(
                stage.at[k, pl.ds(pl.multiple_of(c * ALIGN, ALIGN), ALIGN), :],
                o_ref.at[pl.ds(pl.multiple_of(row * ALIGN, ALIGN), ALIGN), :],
                sem.at[k],
            )

        def drain(step, k):
            def body(_, carry):
                copy16(k, 0, 0).wait()
                return carry

            lax.fori_loop(0, count_ref[step], body, 0)

        def zero_fill(wait):
            def part(p, carry):
                def body(c, carry):
                    d = pltpu.make_async_copy(
                        zeros, o_ref.at[pl.ds(pl.multiple_of(p * CAP + c * ALIGN, ALIGN), ALIGN), :], zsem
                    )
                    d.wait() if wait else d.start()
                    return carry

                return lax.fori_loop(used_ref[p], CAP // ALIGN, body, carry)

            lax.fori_loop(0, parts, part, 0)

        @pl.when(i == 0)
        def _():
            zeros[...] = jnp.zeros_like(zeros)
            zero_fill(False)

        @pl.when(i < tiles)
        def _():
            x = x_ref[...]
            gate = jnp.dot(x, w1_ref[0], preferred_element_type=jnp.float32)
            up = jnp.dot(x, w3_ref[0], preferred_element_type=jnp.float32)
            mid = (jax.nn.silu(gate) * up).astype(jnp.bfloat16)
            out = jnp.dot(mid, w2_ref[0], preferred_element_type=jnp.float32).astype(jnp.bfloat16)

            @pl.when(i >= 2)
            def _():
                drain(i - 2, buf)

            stage[buf] = out

            def body(c, carry):
                copy16(buf, c, dst_ref[i * chunks + c]).start()
                return carry

            lax.fori_loop(0, count_ref[i], body, 0)

        @pl.when(i == tiles_max - 1)
        def _():
            last = tiles - 1

            @pl.when(tiles >= 2)
            def _():
                drain(last - 1, lax.rem(last + 1, 2))

            drain(last, lax.rem(last, 2))
            zero_fill(True)

    def row_block(i, slot, tiles, *_):
        return jnp.minimum(i, tiles[0] - 1), 0

    def slot_block(i, slot, *_):
        return slot[i], 0, 0

    return pl.pallas_call(
        kernel,
        grid_spec=pltpu.PrefetchScalarGridSpec(
            num_scalar_prefetch=5,
            grid=(tiles_max,),
            in_specs=[
                pl.BlockSpec((TM, dim), row_block),
                pl.BlockSpec((1, dim, ff), slot_block),
                pl.BlockSpec((1, dim, ff), slot_block),
                pl.BlockSpec((1, ff, dim), slot_block),
            ],
            out_specs=pl.BlockSpec(memory_space=pl.ANY),
            scratch_shapes=[
                pltpu.VMEM((2, TM, dim), jnp.bfloat16),
                pltpu.VMEM((ALIGN, dim), jnp.bfloat16),
                pltpu.SemaphoreType.DMA((2,)),
                pltpu.SemaphoreType.DMA,
            ],
        ),
        out_shape=jax.ShapeDtypeStruct((out_rows, dim), jnp.bfloat16),
        compiler_params=pltpu.CompilerParams(vmem_limit_bytes=60 * 2**20),
        name="expert_mlp",
    )(tile_slot, num_tiles.reshape(1), chunk_dst, chunk_count, used, x_rows, w1, w3, w2)


def exchange(o_send, plan, turn):
    dim = o_send.shape[1]
    layers, tok, _ = plan.shape
    pieces = dim // PIECE
    units = layers * pieces
    rows = 4 * CAP
    top_k = 6

    def kernel(send_ref, plan_ref, out_ref, recv, zbuf, stage, sel, raw_send, raw_recv, own_sem, z_send, z_recv, out_sem):
        me = lax.axis_index('ep')
        z = me // 4
        q = lax.rem(me, 4)

        def home_of(i):
            low = jnp.where(z == 0, 3 - i, jnp.where(i == 0, 3, jnp.where(i == 1, 0, jnp.where(i == 2, 2, 1))))
            r = 3 - z
            high = jnp.where(r == 0, i, jnp.where(i == 0, 0, jnp.where(i == 1, 3, jnp.where(i == 2, 1, 2))))
            return jnp.where(z < 2, low, high)

        barrier = pltpu.get_barrier_semaphore()
        for d in range(1, 4):
            peer = z * 4 + lax.rem(q + d, 4)
            pl.semaphore_signal(barrier, inc=1, device_id={'ep': peer}, device_id_type=MESH)

        @pl.when(z > 0)
        def _():
            pl.semaphore_signal(barrier, inc=1, device_id={'ep': me - 4}, device_id_type=MESH)

        @pl.when(z < 3)
        def _():
            pl.semaphore_signal(barrier, inc=1, device_id={'ep': me + 4}, device_id_type=MESH)

        pl.semaphore_wait(barrier, 3 + jnp.where(z > 0, 1, 0) + jnp.where(z < 3, 1, 0))

        def block(dst_q, u):
            home, p = home_of(u // pieces), lax.rem(u, pieces)
            row = ((turn * 4 + dst_q) * 4 + home) * CAP
            return send_ref.at[pl.ds(pl.multiple_of(row, ALIGN), CAP), pl.ds(pl.multiple_of(p * PIECE, PIECE), PIECE)]

        def raw(d, u):
            dst_q = lax.rem(q + d, 4)
            return pltpu.make_async_remote_copy(
                src_ref=block(dst_q, u),
                dst_ref=recv.at[u, pl.ds(pl.multiple_of(q * CAP, CAP), CAP), :],
                send_sem=raw_send.at[d - 1, u],
                recv_sem=raw_recv.at[d - 1, u],
                device_id={'ep': z * 4 + dst_q},
                device_id_type=MESH,
            )

        def own(u):
            return pltpu.make_async_copy(
                block(q, u), recv.at[u, pl.ds(pl.multiple_of(q * CAP, CAP), CAP), :], own_sem.at[u]
            )

        def start_raw(u, carry):
            for d in range(1, 4):
                raw(d, u).start()
            own(u).start()
            return carry

        lax.fori_loop(0, units, start_raw, 0)

        def up(slot, u):
            return pltpu.make_async_remote_copy(
                src_ref=stage.at[lax.rem(u, 4)],
                dst_ref=zbuf.at[slot, lax.rem(u, pieces)],
                send_sem=z_send.at[lax.rem(u, 4)],
                recv_sem=z_recv.at[slot, lax.rem(u, pieces)],
                device_id={'ep': me + 4},
                device_id_type=MESH,
            )

        def down(slot, u):
            return pltpu.make_async_remote_copy(
                src_ref=stage.at[lax.rem(u, 4)],
                dst_ref=zbuf.at[slot, lax.rem(u, pieces)],
                send_sem=z_send.at[lax.rem(u, 4)],
                recv_sem=z_recv.at[slot, lax.rem(u, pieces)],
                device_id={'ep': me - 4},
                device_id_type=MESH,
            )

        def finish(u):
            p = lax.rem(u, pieces)
            return pltpu.make_async_copy(
                stage.at[lax.rem(u, 4)], out_ref.at[:, pl.ds(pl.multiple_of(p * PIECE, PIECE), PIECE)], out_sem.at[p]
            )

        def unit(u, carry):
            home, p = home_of(u // pieces), lax.rem(u, pieces)
            k = lax.rem(u, 4)

            @pl.when(p == 0)
            def _():
                lanes = lax.broadcasted_iota(jnp.int32, (tok, CAP), 1).astype(jnp.float32)
                mine = plan_ref[home]
                for src in range(4):
                    a = jnp.zeros((tok, CAP), jnp.float32)
                    for c in range(top_k):
                        a = jnp.where(lanes == mine[:, c : c + 1] - float(src * CAP), mine[:, 8 + c : 9 + c], a)
                    hi = a.astype(jnp.bfloat16)
                    rest = a - hi.astype(jnp.float32)
                    mid = rest.astype(jnp.bfloat16)
                    sel[0, :, src * CAP : (src + 1) * CAP] = hi
                    sel[1, :, src * CAP : (src + 1) * CAP] = mid
                    sel[2, :, src * CAP : (src + 1) * CAP] = (rest - mid.astype(jnp.float32)).astype(jnp.bfloat16)

            for d in range(1, 4):
                raw(d, u).wait()
            own(u).wait()
            o = recv[u]
            acc = jnp.dot(sel[0], o, preferred_element_type=jnp.float32)
            acc += jnp.dot(sel[1], o, preferred_element_type=jnp.float32)
            acc += jnp.dot(sel[2], o, preferred_element_type=jnp.float32)

            @pl.when(u >= 4)
            def _():
                up(0, u - 4).wait_send()

            stage[k] = acc

            @pl.when(((home < z) & (z < 3)) | ((home >= z) & (z > 0)))
            def _():
                up(home, u).wait_recv()
                stage[k] += zbuf[home, p]

            @pl.when((home == z) & (z < 3))
            def _():
                up(4, u).wait_recv()
                stage[k] += zbuf[4, p]

            @pl.when(home > z)
            def _():
                up(home, u).start()

            @pl.when(home < z)
            def _():
                down(jnp.where(home == z - 1, 4, home), u).start()

            @pl.when(home == z)
            def _():
                finish(u).start()

            return carry

        lax.fori_loop(0, units, unit, 0)
        for u in range(units - pieces, units):
            finish(u).wait()

    return pl.pallas_call(
        kernel,
        out_shape=jax.ShapeDtypeStruct((tok, dim), jnp.float32),
        in_specs=[pl.BlockSpec(memory_space=pl.ANY), pl.BlockSpec(memory_space=pltpu.VMEM)],
        out_specs=pl.BlockSpec(memory_space=pl.ANY),
        scratch_shapes=[
            pltpu.VMEM((units, rows, PIECE), jnp.bfloat16),
            pltpu.VMEM((5, pieces, tok, PIECE), jnp.float32),
            pltpu.VMEM((4, tok, PIECE), jnp.float32),
            pltpu.VMEM((3, tok, rows), jnp.bfloat16),
            pltpu.SemaphoreType.DMA((3, units)),
            pltpu.SemaphoreType.DMA((3, units)),
            pltpu.SemaphoreType.DMA((units,)),
            pltpu.SemaphoreType.DMA((4,)),
            pltpu.SemaphoreType.DMA((5, pieces)),
            pltpu.SemaphoreType.DMA((pieces,)),
        ],
        compiler_params=pltpu.CompilerParams(
            collective_id=1 + turn, has_side_effects=True, vmem_limit_bytes=66_000_000
        ),
        name="exchange",
    )(o_send, plan)


def running_count(assign_all, num_slots):
    tok = assign_all.shape[1]
    member = jnp.any(assign_all[..., None] == jnp.arange(num_slots, dtype=jnp.int32), axis=2)
    upto = (jnp.arange(tok)[:, None] >= jnp.arange(tok)[None, :]).astype(jnp.bfloat16)
    order = jnp.einsum('pq,bqs->bps', upto, member.astype(jnp.bfloat16), preferred_element_type=jnp.float32)
    return member, order.astype(jnp.int32)


def solution(mesh):
    group_size = mesh.shape['ep']

    def device_step(x_tokens, slot_expert, w1_slots, w3_slots, w2_slots, assign, w_router, w1_shared, w3_shared, w2_shared):
        tok, dim = x_tokens.shape
        top_k = assign.shape[1]
        slots = w1_slots.shape[0]
        num_slots = slots * group_size
        me = lax.axis_index('ep')
        my_z, my_q = me // 4, me % 4
        max_tiles = slots * (group_size * WIN // TM)
        chunks = TM // ALIGN
        weight = gate_weights(x_tokens, assign, slot_expert, w_router)
        x_all = lax.all_gather(x_tokens, 'ep', tiled=True)
        meta = lax.all_gather(jnp.concatenate([assign.astype(jnp.float32), weight], axis=1), 'ep')
        assign_all = meta[..., :top_k].astype(jnp.int32)
        w_all = meta[..., top_k:]
        shared_out = shared_expert(x_tokens, w1_shared, w3_shared, w2_shared)

        member, order = running_count(assign_all, num_slots)
        count = order[:, -1, :]
        cpad = (count + ALIGN - 1) // ALIGN * ALIGN
        by_dev = cpad.reshape(group_size, group_size, slots)
        crowded = jnp.max(jnp.sum(by_dev, axis=2)) > CAP
        crowded = lax.pmax(crowded.astype(jnp.int32), ('dp', 'ep')) > 0
        split = CAP // WIN
        in_turn = jnp.where(crowded & (jnp.arange(slots) >= split), 1, 0)
        before = jnp.cumsum(by_dev, axis=2) - by_dev
        place = before - jnp.where(in_turn == 1, before[:, :, split : split + 1], 0)
        turn_of = jnp.broadcast_to(in_turn, (group_size, slots)).reshape(num_slots)

        mine = lax.dynamic_slice_in_dim(cpad, me * slots, slots, axis=1)
        my_order = lax.dynamic_slice_in_dim(order, me * slots, slots, axis=2)
        my_member = lax.dynamic_slice_in_dim(member, me * slots, slots, axis=2)
        my_place = lax.dynamic_slice_in_dim(place, me, 1, axis=1)[:, 0]
        tiles = (jnp.sum(mine, axis=0) + TM - 1) // TM
        tile_end = jnp.cumsum(tiles)
        inside = jnp.cumsum(mine, axis=0) - mine
        off = ((tile_end - tiles) * TM)[None, :] + inside
        num_tiles = jnp.maximum(tile_end[-1], 1)
        tile_ids = jnp.arange(max_tiles, dtype=jnp.int32)
        tile_slot = jnp.sum((jnp.minimum(tile_ids, num_tiles - 1)[:, None] >= tile_end[None, :-1]).astype(jnp.int32), axis=1)
        tail = jnp.concatenate([tile_end[:-1], num_tiles[None]]) * TM
        rank = jnp.where(my_member, my_order - 1, -1)
        rank_rows = jnp.pad(jnp.transpose(rank, (0, 2, 1)), ((0, 0), (0, 8 - slots), (0, 0)), constant_values=-1)

        home = jnp.arange(group_size, dtype=jnp.int32)
        base = (in_turn[None, :] * 16 + ((home % 4) * 4 + home // 4)[:, None]) * CAP + my_place
        row0 = jnp.arange(max_tiles * chunks, dtype=jnp.int32) * ALIGN
        lo, hi = off.reshape(-1), (off + mine).reshape(-1)
        inside_group = (row0[:, None] >= lo[None, :]) & (row0[:, None] < hi[None, :])
        chunk_dst = jnp.sum(jnp.where(inside_group, (base - off).reshape(-1)[None, :] + row0[:, None], 0), axis=1) // ALIGN
        chunk_count = jnp.sum(inside_group.reshape(max_tiles, chunks, -1).astype(jnp.int32), axis=(1, 2))
        filled = jnp.stack(
            [jnp.sum(jnp.where(in_turn == 0, mine, 0), axis=1), jnp.where(crowded, jnp.sum(jnp.where(in_turn == 1, mine, 0), axis=1), CAP)]
        )
        used = jnp.transpose(filled.reshape(2, 4, 4), (0, 2, 1)).reshape(-1) // ALIGN

        sum_order = lax.dynamic_slice_in_dim(order.reshape(4, 4, tok, num_slots), my_q, 1, axis=1)[:, 0]
        sum_place = lax.dynamic_slice_in_dim(place.reshape(4, 4, num_slots), my_q, 1, axis=1)[:, 0]
        sum_assign = lax.dynamic_slice_in_dim(assign_all.reshape(4, 4, tok, top_k), my_q, 1, axis=1)[:, 0]
        sum_weight = lax.dynamic_slice_in_dim(w_all.reshape(4, 4, tok, top_k), my_q, 1, axis=1)[:, 0]
        layer_slots = 4 * slots
        slot_ids = jnp.arange(num_slots, dtype=jnp.int32)
        arrives = jnp.where(
            slot_ids // layer_slots == my_z, (slot_ids // slots) % 4 * CAP + sum_place, -(2**20)
        )[:, None, :] + sum_order - 1
        hit = sum_assign[..., None] == slot_ids

        def plan_of(turn):
            col = jnp.sum(jnp.where(hit & (turn_of == turn), arrives[:, :, None, :] + 1, 0), axis=3) - 1
            pad = ((0, 0), (0, 0), (0, 8 - top_k))
            return jnp.concatenate(
                [jnp.pad(col.astype(jnp.float32), pad, constant_values=-1.0), jnp.pad(sum_weight, pad)], axis=2
            )

        x_all, shared_out = lax.optimization_barrier((x_all, shared_out))
        x_rows = dispatch(x_all, rank_rows, off.reshape(-1), mine.reshape(-1), tail, max_tiles * TM)
        o_send = expert_mlp(
            x_rows, w1_slots, w3_slots, w2_slots, tile_slot, num_tiles, chunk_dst, chunk_count, used, 32 * CAP
        )
        routed = exchange(o_send, plan_of(0), 0)
        routed = lax.cond(
            crowded, lambda r, o, p: r + exchange(o, p, 1), lambda r, o, p: r, routed, o_send, plan_of(1)
        )
        return (shared_out + routed).astype(jnp.bfloat16)

    token_spec = P(('dp', 'ep'), None)
    slot_spec = P('ep', None, None)
    return jax.shard_map(device_step, mesh=mesh, in_specs=(token_spec, P(), slot_spec, slot_spec, slot_spec, token_spec, P(), P(), P(), P()), out_specs=token_spec, check_vma=False)
```

time: 1110 us -> 659 us (0.59)
  waiting for transfers between devices: 719 us -> 46.4 us
  Pallas kernels: 241 us -> 452 us
  blocking collectives: 27.2 us -> 65.8 us
  local copies, waits for them, and re-layouts: 39.8 us -> 6.02 us
    reduce_scatter x1 -> x0, waiting for transfers between devices: 632 us -> none  [device_step(): routed = lax.psum_scatter(partial, 'ep', scatter_dimension=0, tiled=True)]
    pallas_call x1, Pallas kernels: 98.7 us -> 329 us  [exchange(): pl.pallas_call(kernel, out_shape=jax.ShapeDtypeStruct((tok, dim), jnp.flo...]
    all_gather x1, waiting for transfers between devices: 86.6 us -> 45.7 us  [device_step(): x_all = lax.all_gather(x_tokens, 'ep', tiled=True)]
    pmax x0 -> x1, blocking collectives: none -> 38.4 us  [device_step(): crowded = lax.pmax(crowded.astype(jnp.int32), ('dp', 'ep')) > 0]
    gather x3 -> x0, local copies, waits for them, and re-layouts: 19 us -> none  [gate_weights(): chosen = jnp.take(slot_expert, jnp.maximum(assign, 0))]
    pallas_call x1, Pallas kernels: 109 us -> 91.6 us  [expert_mlp(): pl.pallas_call(kernel, grid_spec=pltpu.PrefetchScalarGridSpec(num_scalar_...]
  transfers between devices with their start and end apart: 2 -> 1, of which waited for: 2 -> 1; matrix products, arithmetic and copies ran while one was open for 6% -> 9% of each run, Pallas kernels for 0% -> 0%
where the time goes in v2:
time: 659 us; the launch traced here: 649 us
  Pallas kernels  452 us (69%)
  blocking collectives  65.8 us (10%)
  waiting for transfers between devices  46.4 us (7%)
  matrix products  39.6 us (6%)
  other arithmetic  22.6 us (3%)
  between operations  16.2 us (2%)
    pallas_call x1, Pallas kernels, exchange(): pl.pallas_call(kernel, out_shape=jax.ShapeDtypeStruct((tok, dim), jnp.flo...  329 us
    pallas_call x1, Pallas kernels, expert_mlp(): pl.pallas_call(kernel, grid_spec=pltpu.PrefetchScalarGridSpec(num_scalar_...  91.6 us
    all_gather x1, waiting for transfers between devices, device_step(): x_all = lax.all_gather(x_tokens, 'ep', tiled=True)  45.7 us
    pmax x1, blocking collectives, device_step(): crowded = lax.pmax(crowded.astype(jnp.int32), ('dp', 'ep')) > 0  38.4 us
    pallas_call x1, Pallas kernels, dispatch(): pl.pallas_call(kernel, grid_spec=pltpu.PrefetchScalarGridSpec(num_scalar_...  31.6 us
    all_gather x1, blocking collectives, device_step(): lax.all_gather(jnp.concatenate([assign.astype(jnp.float32), weight], axis...  27.4 us
    dot_general x1, matrix products, shared_expert(): return jnp.dot(mid_act, w2_shared, preferred_element_type=jnp.float32)  23.4 us
  transfers between devices with their start and end apart: 1, of which 1 were waited for; matrix products, arithmetic and copies ran while one was open for 9% of the time, Pallas kernels for 0%

profile of v2, /device:TPU:1, one launch (start us, length us, event | category | flops | bytes accessed | tf_op | source)
XLA Modules:
  0.0 648.8 jit_solution(6816286615975989120)
XLA Ops:
  6.5 0.7 all-gather.3.cloned.1.call-update
  7.3 0.7 convert_element_type.43
  8.0 2.6 fusion.18
  10.8 27.4 %all-gather = f32[8192,12]{0,1:T(8,128)S(1)} all-gather(f32[512,12]{0,1:T(8,128)S(1)} %pad_maximum_fusion), channel_id=2, replica_groups=mesh['dp'=2,'ep'=16] {'ep'}, dimensions={0}, use_global_device_ids=true | all-gather | bytes 417792 | tf_op jit(solution)/shard_map/all_gather | solution.py:423
  38.7 5.3 fusion
  44.0 0.9 convolution_convert_fusion
  44.9 1.4 copy-done.3
  47.5 0.6 reduce_max.9
  48.8 38.4 %pmax.7 = s32[]{:T(128)} all-reduce(s32[]{:T(128)S(6)} %convert_element_type.47), channel_id=1, replica_groups=mesh['dp'=2,'ep'=16] {'dp','ep'}, use_global_device_ids=true, to_apply=%region_5.6 | all-reduce | flops 1 | bytes 8 | tf_op jit(solution)/shard_map/pmax | solution.py:433
  89.5 1.1 fusion.24
  90.9 0.6 slice.23
  93.9 1.2 bitcast_add_fusion
  95.1 1.8 select_reduce_fusion
  97.4 0.6 convert_reduce_fusion.1.slot_ref
  98.2 1.5 convert_reduce_fusion.count_ref
  99.6 1.3 select_maximum_fusion.plan_ref
  101.4 0.6 add_select_fusion.2.dst_ref
  102.0 12.8 %fusion.57 = f32[512,2816]{1,0:T(8,128)} fusion(bf16[512,2048]{1,0:T(8,128)(2,1)} %param.12, bf16[2048,2816]{1,0:T(8,128)(2,1)} %param.19), kind=kOutput, calls=%fused_computation.151 | convolution fusion | flops 5905580032 | bytes 19398656 | tf_op jit(solution)/shard_map/dot_general | solution.py:29
  114.9 23.4 %fusion.23 = f32[512,2048]{1,0:T(8,128)} fusion(bf16[2816,2048]{1,0:T(8,128)(2,1)} %param.21, f32[512,2816]{1,0:T(8,128)} %fusion.57, bf16[512,2048]{1,0:T(8,128)(2,1)S(1)} %copy-done.2, bf16[2048,2816]{1,0:T(8,128)(2,1)} %param.20), kind=kOutput, calls=%fused_computation.24 | convolution fusion | flops 11819810816 | bytes 35127296 | tf_op jit(solution)/shard_map/dot_general | solution.py:32
  138.2 45.7 %all-gather.3.cloned.1.call-done.x_ref = bf16[8192,2048]{1,0:T(8,128)(2,1)} async-done(((bf16[512,2048]{1,0:T(8,128)(2,1)}), bf16[8192,2048]{1,0:T(8,128)(2,1)}) %all-gather.3.cloned.1.call-update) | async-done | bytes 33554448 | tf_op jit(solution)/shard_map/all_gather | solution.py:422
  183.9 31.6 %dispatch.1.x_ref = bf16[10240,2048]{1,0:T(8,128)(2,1)} custom-call(s32[80]{0:T(128)S(1)} %ge.71.off_ref, s32[80]{0:T(128)S(1)} %reshape.274.cpad_ref, s32[5]{0:T(128)S(1)} %get-tuple-element.56.tail_ref, s32[16,8,512]{2,1,0:T(8,128)S(1)} %pad.16.rank_ref, bf16[8192,2048]{1,0:T(8,128)(2,1)} %all-gather.3.cloned.1.call-done.x_ref), custom_call_target="tpu_custom_call" | custom-call | tf_op jit(solution)/shard_map/dispatch/pallas_call | solution.py:99
  215.5 91.6 %expert_mlp.1.send_ref = bf16[12288,2048]{1,0:T(8,128)(2,1)} custom-call(s32[40]{0:T(128)} %convert_reduce_fusion.1.slot_ref, s32[1]{0:T(128)} %bitcast.6.tiles_ref, s32[640]{0:T(1024)} %add_select_fusion.2.dst_ref, s32[40]{0:T(128)} %convert_reduce_fusion.count_ref, s32[32]{0:T(128)} %and_select_fusion.4.used_ref, bf16[10240,2048]{1,0:T(8,128)(2,1)} %dispatch.1.x_ref, ...), custom_call_target="tpu_custom_call" | custom-call | tf_op jit(solution)/shard_map/expert_mlp/pallas_call | solution.py:202
  307.1 328.9 %exchange.3 = f32[512,2048]{1,0:T(8,128)} custom-call(bf16[12288,2048]{1,0:T(8,128)(2,1)} %expert_mlp.1.send_ref, f32[4,512,16]{2,1,0:T(8,128)} %select_maximum_fusion.plan_ref), custom_call_target="tpu_custom_call" | custom-call | tf_op jit(solution)/shard_map/exchange/pallas_call | solution.py:377
  636.1 5.4 add_convert_fusion
  (85 shorter events, 6.4 us)
Async XLA Ops:
  6.5 1.4 copy-start
  6.5 4.0 copy-start.4
  6.5 177.4 %all-gather.3.cloned.1.call-start = ((), (), s32[]{:S(2)}) async-start(), calls=%async_computation | async-start | bytes 35651584 | tf_op jit(solution)/shard_map/all_gather | solution.py:422
  44.9 1.4 copy-start.3
  102.0 12.8 %copy-start.2 = (bf16[512,2048]{1,0:T(8,128)(2,1)S(1)}, bf16[512,2048]{1,0:T(8,128)(2,1)}, u32[]{:S(2)}) copy-start(bf16[512,2048]{1,0:T(8,128)(2,1)} %param.12) | copy-start | bytes 6291460
  636.1 5.5 copy-start.1
Sparse Core Ops, SparseCore 0:
  8.9 174.9 all-gather.2

commit v3 on v2

--- a/solution.py
+++ b/solution.py
@@ -8,7 +8,8 @@
 ROUTE_SCALE = 2.5
 TM = 256
 WIN = 128
-ALIGN = 16
+ALIGN = 8
+CHUNKS = (256, 256)
 CAP = 384
 PIECE = 512
 MESH = pl.DeviceIdType.MESH
@@ -119,13 +120,16 @@
     )(off, cpad, tail, rank_rows, x_all)
 
 
-def expert_mlp(x_rows, w1, w3, w2, tile_slot, num_tiles, chunk_dst, chunk_count, used, out_rows):
+def expert_mlp(x_rows, w1, w3, w2, tile_slot, num_tiles, chunk_dst, chunk_count, used, out):
     dim, ff = w1.shape[1:]
+    first = isinstance(out, int)
+    out_rows = out if first else out.shape[0]
     tiles_max = x_rows.shape[0] // TM
     chunks = TM // ALIGN
     parts = out_rows // CAP
 
-    def kernel(slot_ref, tiles_ref, dst_ref, count_ref, used_ref, x_ref, w1_ref, w3_ref, w2_ref, o_ref, stage, zeros, sem, zsem):
+    def kernel(slot_ref, tiles_ref, dst_ref, count_ref, used_ref, x_ref, w1_ref, w3_ref, w2_ref, *rest):
+        o_ref, stage, zeros, sem, zsem = rest[-5:]
         i = pl.program_id(0)
         buf = lax.rem(i, 2)
         tiles = tiles_ref[0]
@@ -157,10 +161,12 @@
 
             lax.fori_loop(0, parts, part, 0)
 
-        @pl.when(i == 0)
-        def _():
-            zeros[...] = jnp.zeros_like(zeros)
-            zero_fill(False)
+        if first:
+
+            @pl.when(i == 0)
+            def _():
+                zeros[...] = jnp.zeros_like(zeros)
+                zero_fill(False)
 
         @pl.when(i < tiles)
         def _():
@@ -191,7 +197,8 @@
                 drain(last - 1, lax.rem(last + 1, 2))
 
             drain(last, lax.rem(last, 2))
-            zero_fill(True)
+            if first:
+                zero_fill(True)
 
     def row_block(i, slot, tiles, *_):
         return jnp.minimum(i, tiles[0] - 1), 0
@@ -209,7 +216,8 @@
                 pl.BlockSpec((1, dim, ff), slot_block),
                 pl.BlockSpec((1, dim, ff), slot_block),
                 pl.BlockSpec((1, ff, dim), slot_block),
-            ],
+            ]
+            + ([] if first else [pl.BlockSpec(memory_space=pl.ANY)]),
             out_specs=pl.BlockSpec(memory_space=pl.ANY),
             scratch_shapes=[
                 pltpu.VMEM((2, TM, dim), jnp.bfloat16),
@@ -220,16 +228,17 @@
         ),
         out_shape=jax.ShapeDtypeStruct((out_rows, dim), jnp.bfloat16),
         compiler_params=pltpu.CompilerParams(vmem_limit_bytes=60 * 2**20),
+        input_output_aliases={} if first else {9: 0},
         name="expert_mlp",
-    )(tile_slot, num_tiles.reshape(1), chunk_dst, chunk_count, used, x_rows, w1, w3, w2)
-
-
-def exchange(o_send, plan, turn):
+    )(tile_slot, num_tiles.reshape(1), chunk_dst, chunk_count, used, x_rows, w1, w3, w2, *([] if first else [out]))
+
+
+def exchange(o_send, plan, turn, cap):
     dim = o_send.shape[1]
     layers, tok, _ = plan.shape
     pieces = dim // PIECE
     units = layers * pieces
-    rows = 4 * CAP
+    rows = 4 * cap
     top_k = 6
 
     def kernel(send_ref, plan_ref, out_ref, recv, zbuf, stage, sel, raw_send, raw_recv, own_sem, z_send, z_recv, out_sem):
@@ -261,13 +270,13 @@
         def block(dst_q, u):
             home, p = home_of(u // pieces), lax.rem(u, pieces)
             row = ((turn * 4 + dst_q) * 4 + home) * CAP
-            return send_ref.at[pl.ds(pl.multiple_of(row, ALIGN), CAP), pl.ds(pl.multiple_of(p * PIECE, PIECE), PIECE)]
+            return send_ref.at[pl.ds(pl.multiple_of(row, 128), cap), pl.ds(pl.multiple_of(p * PIECE, PIECE), PIECE)]
 
         def raw(d, u):
             dst_q = lax.rem(q + d, 4)
             return pltpu.make_async_remote_copy(
                 src_ref=block(dst_q, u),
-                dst_ref=recv.at[u, pl.ds(pl.multiple_of(q * CAP, CAP), CAP), :],
+                dst_ref=recv.at[u, pl.ds(pl.multiple_of(q * cap, cap), cap), :],
                 send_sem=raw_send.at[d - 1, u],
                 recv_sem=raw_recv.at[d - 1, u],
                 device_id={'ep': z * 4 + dst_q},
@@ -276,7 +285,7 @@
 
         def own(u):
             return pltpu.make_async_copy(
-                block(q, u), recv.at[u, pl.ds(pl.multiple_of(q * CAP, CAP), CAP), :], own_sem.at[u]
+                block(q, u), recv.at[u, pl.ds(pl.multiple_of(q * cap, cap), cap), :], own_sem.at[u]
             )
 
         def start_raw(u, carry):
@@ -319,32 +328,34 @@
 
             @pl.when(p == 0)
             def _():
-                lanes = lax.broadcasted_iota(jnp.int32, (tok, CAP), 1).astype(jnp.float32)
+                lanes = lax.broadcasted_iota(jnp.int32, (tok, cap), 1).astype(jnp.float32)
                 mine = plan_ref[home]
                 for src in range(4):
-                    a = jnp.zeros((tok, CAP), jnp.float32)
+                    a = jnp.zeros((tok, cap), jnp.float32)
                     for c in range(top_k):
-                        a = jnp.where(lanes == mine[:, c : c + 1] - float(src * CAP), mine[:, 8 + c : 9 + c], a)
+                        a = jnp.where(lanes == mine[:, c : c + 1] - float(src * cap), mine[:, 8 + c : 9 + c], a)
                     hi = a.astype(jnp.bfloat16)
                     rest = a - hi.astype(jnp.float32)
                     mid = rest.astype(jnp.bfloat16)
-                    sel[0, :, src * CAP : (src + 1) * CAP] = hi
-                    sel[1, :, src * CAP : (src + 1) * CAP] = mid
-                    sel[2, :, src * CAP : (src + 1) * CAP] = (rest - mid.astype(jnp.float32)).astype(jnp.bfloat16)
+                    sel[0, :, src * cap : (src + 1) * cap] = hi
+                    sel[1, :, src * cap : (src + 1) * cap] = mid
+                    sel[2, :, src * cap : (src + 1) * cap] = (rest - mid.astype(jnp.float32)).astype(jnp.bfloat16)
 
             for d in range(1, 4):
                 raw(d, u).wait()
             own(u).wait()
-            o = recv[u]
-            acc = jnp.dot(sel[0], o, preferred_element_type=jnp.float32)
-            acc += jnp.dot(sel[1], o, preferred_element_type=jnp.float32)
-            acc += jnp.dot(sel[2], o, preferred_element_type=jnp.float32)
 
             @pl.when(u >= 4)
             def _():
                 up(0, u - 4).wait_send()
 
-            stage[k] = acc
+            stage[k] = jnp.dot(sel[0], recv[u], preferred_element_type=jnp.float32)
+
+            def term(j, c):
+                stage[k] += jnp.dot(sel[j], recv[u], preferred_element_type=jnp.float32)
+                return c
+
+            lax.fori_loop(1, 3, term, 0)
 
             @pl.when(((home < z) & (z < 3)) | ((home >= z) & (z > 0)))
             def _():
@@ -419,77 +430,99 @@
         max_tiles = slots * (group_size * WIN // TM)
         chunks = TM // ALIGN
         weight = gate_weights(x_tokens, assign, slot_expert, w_router)
-        x_all = lax.all_gather(x_tokens, 'ep', tiled=True)
-        meta = lax.all_gather(jnp.concatenate([assign.astype(jnp.float32), weight], axis=1), 'ep')
-        assign_all = meta[..., :top_k].astype(jnp.int32)
-        w_all = meta[..., top_k:]
-        shared_out = shared_expert(x_tokens, w1_shared, w3_shared, w2_shared)
+        ends = [sum(CHUNKS[: c + 1]) for c in range(len(CHUNKS))]
+        x_chunks = [lax.all_gather(x_tokens[e - t : e], 'ep', tiled=True) for t, e in zip(CHUNKS, ends)]
+        meta = lax.all_gather(jnp.concatenate([assign.astype(jnp.float32), weight], axis=1), ('dp', 'ep'))
+        meta = meta.reshape(-1, group_size, tok, 2 * top_k)
+        everyone = meta[..., :top_k].astype(jnp.int32)
+        my_dp = lax.axis_index('dp')
+        assign_all = lax.dynamic_index_in_dim(everyone, my_dp, 0, keepdims=False)
+        w_all = lax.dynamic_index_in_dim(meta, my_dp, 0, keepdims=False)[..., top_k:]
+
+        def padded(count):
+            return (count + ALIGN - 1) // ALIGN * ALIGN
+
+        member_e = jnp.any(everyone[..., None] == jnp.arange(num_slots, dtype=jnp.int32), axis=3)
+        need = sum(
+            jnp.sum(padded(jnp.sum(member_e[:, :, e - t : e].astype(jnp.int32), axis=2)).reshape(-1, group_size, slots), axis=2)
+            for t, e in zip(CHUNKS, ends)
+        )
+        crowded = jnp.max(need) > CAP
 
         member, order = running_count(assign_all, num_slots)
-        count = order[:, -1, :]
-        cpad = (count + ALIGN - 1) // ALIGN * ALIGN
-        by_dev = cpad.reshape(group_size, group_size, slots)
-        crowded = jnp.max(jnp.sum(by_dev, axis=2)) > CAP
-        crowded = lax.pmax(crowded.astype(jnp.int32), ('dp', 'ep')) > 0
+        totals = jnp.stack([order[:, e - 1, :] for e in ends])
+        starts = jnp.concatenate([jnp.zeros_like(totals[:1]), totals[:-1]])
+        cpad = padded(totals - starts)
+        by_dev = jnp.transpose(cpad.reshape(len(CHUNKS), group_size, group_size, slots), (1, 2, 3, 0))
         split = CAP // WIN
         in_turn = jnp.where(crowded & (jnp.arange(slots) >= split), 1, 0)
-        before = jnp.cumsum(by_dev, axis=2) - by_dev
-        place = before - jnp.where(in_turn == 1, before[:, :, split : split + 1], 0)
+        flat = by_dev.reshape(group_size, group_size, -1)
+        before = (jnp.cumsum(flat, axis=2) - flat).reshape(by_dev.shape)
+        place = before - jnp.where(in_turn[:, None] == 1, before[:, :, split : split + 1, :1], 0)
+        place = jnp.transpose(place, (3, 0, 1, 2))
         turn_of = jnp.broadcast_to(in_turn, (group_size, slots)).reshape(num_slots)
 
-        mine = lax.dynamic_slice_in_dim(cpad, me * slots, slots, axis=1)
+        my_pad = lax.dynamic_slice_in_dim(cpad, me * slots, slots, axis=2)
+        my_start = lax.dynamic_slice_in_dim(starts, me * slots, slots, axis=2)
         my_order = lax.dynamic_slice_in_dim(order, me * slots, slots, axis=2)
         my_member = lax.dynamic_slice_in_dim(member, me * slots, slots, axis=2)
-        my_place = lax.dynamic_slice_in_dim(place, me, 1, axis=1)[:, 0]
-        tiles = (jnp.sum(mine, axis=0) + TM - 1) // TM
-        tile_end = jnp.cumsum(tiles)
-        inside = jnp.cumsum(mine, axis=0) - mine
-        off = ((tile_end - tiles) * TM)[None, :] + inside
-        num_tiles = jnp.maximum(tile_end[-1], 1)
+        my_place = lax.dynamic_slice_in_dim(place, me, 1, axis=2)[:, :, 0]
+        home = jnp.arange(group_size, dtype=jnp.int32)
+        base = (in_turn[None, :] * 16 + ((home % 4) * 4 + home // 4)[:, None]) * CAP
         tile_ids = jnp.arange(max_tiles, dtype=jnp.int32)
-        tile_slot = jnp.sum((jnp.minimum(tile_ids, num_tiles - 1)[:, None] >= tile_end[None, :-1]).astype(jnp.int32), axis=1)
-        tail = jnp.concatenate([tile_end[:-1], num_tiles[None]]) * TM
-        rank = jnp.where(my_member, my_order - 1, -1)
-        rank_rows = jnp.pad(jnp.transpose(rank, (0, 2, 1)), ((0, 0), (0, 8 - slots), (0, 0)), constant_values=-1)
-
-        home = jnp.arange(group_size, dtype=jnp.int32)
-        base = (in_turn[None, :] * 16 + ((home % 4) * 4 + home // 4)[:, None]) * CAP + my_place
         row0 = jnp.arange(max_tiles * chunks, dtype=jnp.int32) * ALIGN
-        lo, hi = off.reshape(-1), (off + mine).reshape(-1)
-        inside_group = (row0[:, None] >= lo[None, :]) & (row0[:, None] < hi[None, :])
-        chunk_dst = jnp.sum(jnp.where(inside_group, (base - off).reshape(-1)[None, :] + row0[:, None], 0), axis=1) // ALIGN
-        chunk_count = jnp.sum(inside_group.reshape(max_tiles, chunks, -1).astype(jnp.int32), axis=(1, 2))
+
+        def chunk_plan(c):
+            t, e, mine = CHUNKS[c], ends[c], my_pad[c]
+            tiles = (jnp.sum(mine, axis=0) + TM - 1) // TM
+            tile_end = jnp.cumsum(tiles)
+            off = ((tile_end - tiles) * TM)[None, :] + jnp.cumsum(mine, axis=0) - mine
+            num_tiles = jnp.maximum(tile_end[-1], 1)
+            tile_slot = jnp.sum((jnp.minimum(tile_ids, num_tiles - 1)[:, None] >= tile_end[None, :-1]).astype(jnp.int32), axis=1)
+            tail = jnp.concatenate([tile_end[:-1], num_tiles[None]]) * TM
+            rank = jnp.where(my_member[:, e - t : e], my_order[:, e - t : e] - my_start[c][:, None, :] - 1, -1)
+            rank_rows = jnp.pad(jnp.transpose(rank, (0, 2, 1)), ((0, 0), (0, 8 - slots), (0, 0)), constant_values=-1)
+            lo, hi = off.reshape(-1), (off + mine).reshape(-1)
+            inside = (row0[:, None] >= lo[None, :]) & (row0[:, None] < hi[None, :])
+            shift = (base + my_place[c] - off).reshape(-1)
+            dst = jnp.sum(jnp.where(inside, shift[None, :] + row0[:, None], 0), axis=1) // ALIGN
+            count = jnp.sum(inside.reshape(max_tiles, chunks, -1).astype(jnp.int32), axis=(1, 2))
+            return (rank_rows, off.reshape(-1), mine.reshape(-1), tail), (tile_slot, num_tiles, dst, count)
+
+        mine = jnp.sum(my_pad, axis=0)
         filled = jnp.stack(
             [jnp.sum(jnp.where(in_turn == 0, mine, 0), axis=1), jnp.where(crowded, jnp.sum(jnp.where(in_turn == 1, mine, 0), axis=1), CAP)]
         )
         used = jnp.transpose(filled.reshape(2, 4, 4), (0, 2, 1)).reshape(-1) // ALIGN
 
         sum_order = lax.dynamic_slice_in_dim(order.reshape(4, 4, tok, num_slots), my_q, 1, axis=1)[:, 0]
-        sum_place = lax.dynamic_slice_in_dim(place.reshape(4, 4, num_slots), my_q, 1, axis=1)[:, 0]
+        sum_place = lax.dynamic_slice_in_dim((place.reshape(starts.shape) - starts).reshape(-1, 4, 4, num_slots), my_q, 1, axis=2)[:, :, 0]
         sum_assign = lax.dynamic_slice_in_dim(assign_all.reshape(4, 4, tok, top_k), my_q, 1, axis=1)[:, 0]
         sum_weight = lax.dynamic_slice_in_dim(w_all.reshape(4, 4, tok, top_k), my_q, 1, axis=1)[:, 0]
-        layer_slots = 4 * slots
         slot_ids = jnp.arange(num_slots, dtype=jnp.int32)
-        arrives = jnp.where(
-            slot_ids // layer_slots == my_z, (slot_ids // slots) % 4 * CAP + sum_place, -(2**20)
-        )[:, None, :] + sum_order - 1
+        arrives = jnp.where(slot_ids // (4 * slots) == my_z, (slot_ids // slots) % 4 * CAP + sum_place, -(2**20))
+        arrives = jnp.concatenate(
+            [jnp.broadcast_to(arrives[c][:, None, :], (4, t, num_slots)) for c, t in enumerate(CHUNKS)], axis=1
+        ) + sum_order
         hit = sum_assign[..., None] == slot_ids
 
         def plan_of(turn):
-            col = jnp.sum(jnp.where(hit & (turn_of == turn), arrives[:, :, None, :] + 1, 0), axis=3) - 1
+            col = jnp.sum(jnp.where(hit & (turn_of == turn), arrives[:, :, None, :], 0), axis=3) - 1
             pad = ((0, 0), (0, 0), (0, 8 - top_k))
             return jnp.concatenate(
                 [jnp.pad(col.astype(jnp.float32), pad, constant_values=-1.0), jnp.pad(sum_weight, pad)], axis=2
             )
 
-        x_all, shared_out = lax.optimization_barrier((x_all, shared_out))
-        x_rows = dispatch(x_all, rank_rows, off.reshape(-1), mine.reshape(-1), tail, max_tiles * TM)
-        o_send = expert_mlp(
-            x_rows, w1_slots, w3_slots, w2_slots, tile_slot, num_tiles, chunk_dst, chunk_count, used, 32 * CAP
-        )
-        routed = exchange(o_send, plan_of(0), 0)
+        plans = [chunk_plan(c) for c in range(len(CHUNKS))]
+        shared_out = shared_expert(x_tokens, w1_shared, w3_shared, w2_shared)
+        x_chunks[0], shared_out = lax.optimization_barrier((x_chunks[0], shared_out))
+        o_send = 32 * CAP
+        for x_part, (rows_plan, tiles_plan) in zip(x_chunks, plans):
+            x_rows = dispatch(x_part, *rows_plan, max_tiles * TM)
+            o_send = expert_mlp(x_rows, w1_slots, w3_slots, w2_slots, *tiles_plan, used, o_send)
+        routed = exchange(o_send, plan_of(0), 0, CAP)
         routed = lax.cond(
-            crowded, lambda r, o, p: r + exchange(o, p, 1), lambda r, o, p: r, routed, o_send, plan_of(1)
+            crowded, lambda r, o, p: r + exchange(o, p, 1, CAP), lambda r, o, p: r, routed, o_send, plan_of(1)
         )
         return (shared_out + routed).astype(jnp.bfloat16)
 

time: 659 us -> 686 us (1.041)
  the two profiles are of different devices: /device:TPU:1 before, /device:TPU:31 now
where the time goes in v3:
time: 686 us; the launch traced here: 679 us
  Pallas kernels  484 us (71%)
  blocking collectives  43.8 us (6%)
  other arithmetic  42.9 us (6%)
  matrix products  36.5 us (5%)
  waiting for transfers between devices  35.2 us (5%)
  local copies, waits for them, and re-layouts  20.1 us (3%)
  between operations  16.4 us (2%)
    pallas_call x1, Pallas kernels, exchange(): pl.pallas_call(kernel, out_shape=jax.ShapeDtypeStruct((tok, dim), jnp.flo...  323 us
    pallas_call x2, Pallas kernels, expert_mlp(): pl.pallas_call(kernel, grid_spec=pltpu.PrefetchScalarGridSpec(num_scalar_...  119 us
    all_gather x1, blocking collectives, device_step(): lax.all_gather(jnp.concatenate([assign.astype(jnp.float32), weight], axis...  43.8 us
    pallas_call x2, Pallas kernels, dispatch(): pl.pallas_call(kernel, grid_spec=pltpu.PrefetchScalarGridSpec(num_scalar_...  42.4 us
    all_gather x2, waiting for transfers between devices, device_step(): lax.all_gather(x_tokens[e - t:e], 'ep', tiled=True)  34.5 us
    dot_general x1, matrix products, shared_expert(): return jnp.dot(mid_act, w2_shared, preferred_element_type=jnp.float32)  23.4 us
  transfers between devices with their start and end apart: 2, of which 1 were waited for; matrix products, arithmetic and copies ran while one was open for 13% of the time, Pallas kernels for 12%

profile of v3, /device:TPU:31, one launch (start us, length us, event | category | flops | bytes accessed | tf_op | source)
XLA Modules:
  0.0 679.3 jit_solution(11853274830230487101)
XLA Ops:
  6.6 3.3 fusion.61
  11.9 43.8 %all-gather = f32[16384,12]{0,1:T(8,128)S(1)} all-gather(f32[512,12]{0,1:T(8,128)S(1)} %pad_maximum_fusion), channel_id=2, replica_groups=mesh['dp'=2,'ep'=16] {'dp','ep'}, dimensions={0}, use_global_device_ids=true | all-gather | bytes 811008 | tf_op jit(solution)/shard_map/all_gather | solution.py:435
  57.8 11.7 %fusion = pred[2,16,512,80]{2,3,1,0:T(8,128)(4,1)S(1)} fusion(s32[2,16,512,6]{2,3,1,0:T(8,128)S(1)} %copy.166), kind=kLoop, calls=%fused_computation.1 | loop fusion | flops 14417920 | bytes 1703936 | tf_op jit(solution)/shard_map/reduce_or | solution.py:445
  69.5 1.2 convert_reduce_fusion
  74.0 1.4 copy.201
  75.4 1.3 pad.23
  77.6 5.2 fusion.1
  83.7 1.5 copy-done.3
  96.0 1.2 add_add_fusion
  97.2 3.1 select_reduce_fusion
  100.4 1.4 copy.189
  103.3 1.5 select_maximum_fusion.1
  104.8 2.5 select_maximum_fusion.plan_ref
  108.0 2.3 convert_reduce_fusion.2
  110.6 1.3 and_select_fusion.5.used_ref
  113.0 11.3 %fusion.64 = f32[512,2816]{1,0:T(8,128)} fusion(bf16[512,2048]{1,0:T(8,128)(2,1)S(1)} %copy-done.2, bf16[2048,2816]{1,0:T(8,128)(2,1)} %param.19), kind=kOutput, calls=%fused_computation.195 | convolution fusion | flops 5905580032 | bytes 19398656 | tf_op jit(solution)/shard_map/dot_general | solution.py:30
  124.3 23.4 %fusion.24 = f32[512,2048]{1,0:T(8,128)} fusion(bf16[2816,2048]{1,0:T(8,128)(2,1)} %param.21, f32[512,2816]{1,0:T(8,128)} %fusion.64, bf16[512,2048]{1,0:T(8,128)(2,1)S(1)} %copy-done.2, bf16[2048,2816]{1,0:T(8,128)(2,1)} %param.20), kind=kOutput, calls=%fused_computation.28 | convolution fusion | flops 11819810816 | bytes 35127296 | tf_op jit(solution)/shard_map/dot_general | solution.py:33
  147.7 21.2 %dispatch.3.x_ref = bf16[10240,2048]{1,0:T(8,128)(2,1)} custom-call(s32[80]{0:T(128)S(1)} %get-tuple-element.69.off_ref, s32[80]{0:T(128)S(1)} %squeeze.38.cpad_ref, s32[5]{0:T(128)S(1)} %get-tuple-element.72.tail_ref, s32[16,8,256]{2,1,0:T(8,128)S(1)} %pad.21.rank_ref, bf16[4096,2048]{1,0:T(8,128)(2,1)} %all-gather.4.cloned.1.call-done.x_ref), custom_call_target="tpu_custom_call" | custom-call | tf_op jit(solution)/shard_map/dispatch/pallas_call | solution.py:100
  168.9 62.5 %expert_mlp.2.rest_0_ = bf16[12288,2048]{1,0:T(8,128)(2,1)} custom-call(s32[40]{0:T(128)} %get-tuple-element.70.slot_ref, s32[1]{0:T(128)} %bitcast.23.tiles_ref, s32[1280]{0:T(1024)} %add_select_fusion.3.dst_ref, s32[40]{0:T(128)} %get-tuple-element.42.count_ref, s32[32]{0:T(128)} %and_select_fusion.5.used_ref, bf16[10240,2048]{1,0:T(8,128)(2,1)} %dispatch.3.x_ref, ...), custom_call_target="tpu_custom_call" | custom-call | tf_op jit(solution)/shard_map/expert_mlp/pallas_call | solution.py:209
  231.4 34.5 %all-gather.6.cloned.1.call-done.x_ref = bf16[4096,2048]{1,0:T(8,128)(2,1)} async-done(((bf16[256,2048]{1,0:T(8,128)(2,1)}), bf16[4096,2048]{1,0:T(8,128)(2,1)}) %all-gather.6.cloned.1.call-update) | async-done | bytes 16777232 | tf_op jit(solution)/shard_map/all_gather | solution.py:434
  265.9 21.2 %dispatch.2.x_ref = bf16[10240,2048]{1,0:T(8,128)(2,1)} custom-call(s32[80]{0:T(128)S(1)} %get-tuple-element.49.off_ref, s32[80]{0:T(128)S(1)} %squeeze.35.cpad_ref, s32[5]{0:T(128)S(1)} %add_multiply_fusion.2.tail_ref, s32[16,8,256]{2,1,0:T(8,128)S(1)} %pad.20.rank_ref, bf16[4096,2048]{1,0:T(8,128)(2,1)} %all-gather.6.cloned.1.call-done.x_ref), custom_call_target="tpu_custom_call" | custom-call | tf_op jit(solution)/shard_map/dispatch/pallas_call | solution.py:100
  287.1 56.7 %expert_mlp.3.send_ref = bf16[12288,2048]{1,0:T(8,128)(2,1)} custom-call(s32[40]{0:T(128)} %get-tuple-element.71.slot_ref, s32[1]{0:T(128)} %bitcast.7.tiles_ref, s32[1280]{0:T(1024)} %add_select_fusion.4.dst_ref, s32[40]{0:T(128)} %get-tuple-element.43.count_ref, s32[32]{0:T(128)} %and_select_fusion.5.used_ref, ...), custom_call_target="tpu_custom_call", output_to_operand_aliasing={{}: (9, {})} | custom-call | tf_op jit(solution)/shard_map/expert_mlp/pallas_call | solution.py:209
  343.9 322.7 %exchange.3 = f32[512,2048]{1,0:T(8,128)} custom-call(bf16[12288,2048]{1,0:T(8,128)(2,1)} %expert_mlp.3.send_ref, f32[4,512,16]{2,1,0:T(8,128)} %select_maximum_fusion.plan_ref), custom_call_target="tpu_custom_call" | custom-call | tf_op jit(solution)/shard_map/exchange/pallas_call | solution.py:388
  666.6 5.4 add_convert_fusion
  (137 shorter events, 21.5 us)
Async XLA Ops:
  6.5 4.2 copy-start
  6.5 4.2 copy-start.2
  6.5 4.1 copy-start.7
  6.5 4.2 copy-start.11
  6.5 141.1 %all-gather.4.cloned.1.call-start = ((), (), s32[]{:S(2)}) async-start(), calls=%async_computation | async-start | bytes 17825792 | tf_op jit(solution)/shard_map/all_gather | solution.py:434
  9.9 256.0 %all-gather.6.cloned.1.call-start = ((), (), s32[]{:S(2)}) async-start(), calls=%async_computation.1 | async-start | bytes 17825792 | tf_op jit(solution)/shard_map/all_gather | solution.py:434
  82.8 3.4 copy-start.4
  83.7 1.5 copy-start.3
  83.7 13.5 %copy-start.6 = (s32[4,1,512,6]{2,3,0,1:T(8,128)S(1)}, s32[4,1,512,6]{2,3,0,1:T(8,128)}, u32[]{:S(2)}) copy-start(s32[4,1,512,6]{2,3,0,1:T(8,128)} %copy.208) | copy-start | bytes 147460
  88.8 2.0 copy-start.9
  93.0 8.7 %copy-start.10 = (s32[5,1]{0,1:T(1,128)S(1)}, s32[5,1]{0,1:T(1,128)}, u32[]{:S(2)}) copy-start(s32[5,1]{0,1:T(1,128)} %copy-done.9) | copy-start | bytes 64
  95.8 11.6 %copy-start.8 = (s32[80]{0:T(128)S(1)}, s32[80]{0:T(128)}, u32[]{:S(2)}) copy-start(s32[80]{0:T(128)} %squeeze.36) | copy-start | bytes 964
  343.9 322.7 %copy-start.5 = (f32[4,512,16]{1,2,0:T(8,128)S(1)}, f32[4,512,16]{1,2,0:T(8,128)}, u32[]{:S(2)}) copy-start(f32[4,512,16]{1,2,0:T(8,128)} %select_maximum_fusion.1) | copy-start | bytes 393220
  666.6 5.5 copy-start.1
Sparse Core Ops, SparseCore 0:
  10.0 129.2 all-gather.3
  141.4 124.3 all-gather.5
